TPU v7x, 128 devices: a whole 4x4x4 slice. The times are simulated.
128 devices in a mesh: dp: 1, yax: 16 (over z, y), xax: 8 (over x, core).
Axes of the slice: x: 4, y: 4, z: 4, core: 2. Of those that a mesh axis runs over, the one named last changes fastest.
Arguments:
- hidden: bfloat16 [768, 4096], P('dp', 'xax')
- cache_len: int32 [768], P('dp')
- k_cache: bfloat16 [768, 1024, 128], P(('dp', 'yax', 'xax'))
- v_cache: bfloat16 [768, 1024, 128], P(('dp', 'yax', 'xax'))
- g_attn: float32 [4096], P('xax')
- w_query: bfloat16 [4096, 4096], P('xax', 'yax')
- w_key: bfloat16 [4096, 128], P('xax')
- w_value: bfloat16 [4096, 128], P('xax')
- w_gate: bfloat16 [4096, 16384], P('xax', 'yax')
- w_up: bfloat16 [4096, 16384], P('xax', 'yax')
- w_out: bfloat16 [4096, 4096], P('yax', 'xax')
- w_down: bfloat16 [16384, 4096], P('yax', 'xax')
- g_final: float32 [4096], P('xax')
- embedding: bfloat16 [50432, 4096], P('yax', 'xax')
Outputs:
- output 1: bfloat16 [768, 128], P(('dp', 'yax', 'xax'))
- output 2: bfloat16 [768, 128], P(('dp', 'yax', 'xax'))
- output 3: float32 [768, 50432], P('dp', ('yax', 'xax'))
- output 4: float32 [768], P('dp')
All inputs are finite; a program needn't handle non-finite values.
Results may differ from a plain program's by a relative error of at most 0.00127.
Values are sent between devices in bfloat16 or wider.
A program may use at most 1 GiB of HBM per device.

v0:
```python
import contextlib
import itertools

import jax
import jax.numpy as jnp
import numpy as np
from jax import lax
from jax.experimental import pallas as pl
from jax.experimental.pallas import tpu as pltpu
from jax.sharding import PartitionSpec as P

EPS = 1e-6
ROPE_BASE = 10000.0
MESH_ID = pl.DeviceIdType.MESH
NY = NZ = NX = 4
CORES = 2
POOL, SENDS, TAGS = 24, 59, 86
HOPS = (1, 3, 2)
FAR_FIRST = (2, 1, 3)
LINE = [(0, 1), (1, 0), (3, 0), (1, 1), (3, 1), (2, 0), (2, 1)]
NEAR = LINE[1:5]
NT = (((1,), (1,)), ((), ()))
PLANE = [(dz, dy) for dz in range(NZ) for dy in range(NY) if dz or dy]


class Group:
    def __init__(self, links, whole):
        self.links, self.whole = links, whole
        self.tag, self.sem = next(links.tags), next(links.slow)
        links.groups.append(self)

    def send(self, src, dst, where):
        pltpu.make_async_remote_copy(
            src_ref=src, dst_ref=dst, send_sem=self.links.send_sem.at[self.sem],
            recv_sem=self.links.recv_sem.at[self.tag], device_id=where, device_id_type=MESH_ID).start()

    def wait(self):
        pltpu.make_async_copy(self.whole, self.whole, self.links.recv_sem.at[self.tag]).wait()

    def wait_sent(self):
        pltpu.make_async_copy(self.whole, self.whole, self.links.send_sem.at[self.sem]).wait()


class Phases:
    def __init__(self):
        self.stack = contextlib.ExitStack()

    def __call__(self, name):
        self.close()
        self.stack.enter_context(jax.named_scope(name))

    def close(self):
        self.stack.close()


class Links:
    def __init__(self, send_sem, recv_sem):
        self.send_sem, self.recv_sem = send_sem, recv_sem
        self.tags, self.slow, self.fast = itertools.count(), itertools.count(POOL), []
        self.pending, self.groups = [], []
        self.y_idx = lax.axis_index("yax")
        self.x_idx = lax.axis_index("xax")
        self.z, self.y = self.y_idx // NY, self.y_idx % NY
        self.chip, self.core = self.x_idx // CORES, self.x_idx % CORES

    def at_plane(self, dz, dy):
        return {"yax": (self.z + dz) % NZ * NY + (self.y + dy) % NY, "xax": self.x_idx}

    def slot_rows(self, dz, dy, rows):
        slot = (self.z + dz) % NZ * NY + (self.y + dy) % NY
        return pl.ds(pl.multiple_of(slot * rows, rows), rows)

    def line_id(self, dx, oc):
        core = 1 - self.core if oc else self.core
        return (self.chip + dx) % NX * CORES + core

    def at_line(self, dx, oc):
        return {"yax": self.y_idx, "xax": self.line_id(dx, oc)}

    def send(self, src, dst, where, tag=None, long=False):
        tag = next(self.tags) if tag is None else tag
        if long:
            sem = next(self.slow)
        else:
            sem = len(self.fast) % POOL
            if len(self.fast) >= POOL:
                self.fast[-POOL].wait_send()
        copy = pltpu.make_async_remote_copy(
            src_ref=src, dst_ref=dst, send_sem=self.send_sem.at[sem], recv_sem=self.recv_sem.at[tag],
            device_id=where, device_id_type=MESH_ID)
        copy.start()
        (self.pending if long else self.fast).append(copy)
        return copy

    def finish(self):
        for copy in self.pending + self.fast[-POOL:]:
            copy.wait_send()
        for group in self.groups:
            group.wait_sent()

    def barrier(self):
        barrier = pltpu.get_barrier_semaphore()
        peers = [self.at_line(*p) for p in LINE] + [self.at_plane(*p) for p in PLANE]
        for peer in peers:
            pl.semaphore_signal(barrier, inc=1, device_id=peer, device_id_type=MESH_ID)
        pl.semaphore_wait(barrier, len(peers))


def lane_sum(v):
    return jnp.sum(v, axis=-1, keepdims=True)


def plane_gather(links, buf, tags, hook, crossing, start):
    cols = buf.shape[-1]
    rows = buf.shape[1] // (NY * NZ)
    span = (cols - start) // 2
    partner = links.at_line(0, 1)

    class Part:
        def __init__(self, index):
            self.index, self.lo, self.got = index, start + index * span, {}

        def order(self, du, dv):
            return (du, dv) if self.index else (dv, du)

        def block(self, at, half=0, piece=None):
            width = span if piece is None else span // 2
            lo = self.lo if not piece else self.lo + width
            return buf.at[half, links.slot_rows(*self.order(*at), rows), pl.ds(lo, width)]

        def push(self, name, at, to, piece=None):
            ref = self.block(at, piece=piece)
            self.got[name] = links.send(ref, ref, links.at_plane(*self.order(*to)), next(tags))

        def spread(self, k, at):
            self.push(("v+", k), at, (0, 1))
            self.push(("v-", k), at, (0, -1))

        def give(self, at):
            crossing.send(self.block(at), self.block(at, half=1), partner)

        def wait(self, name):
            self.got[name].wait_recv()

    parts = [Part(index) for index in range(2)]
    offset = (0, -1, 1, 2)
    for p in parts:
        p.push("u+", (0, 0), (1, 0))
        p.push("u-", (0, 0), (-1, 0))
        p.spread(0, (0, 0))
    for p in parts:
        p.give((0, 0))
    for k, name in enumerate(("u+", "u-"), 1):
        for p in parts:
            p.wait(name)
            at = (offset[k], 0)
            p.push(("far", k), at, (-offset[k], 0), piece=k - 1)
            p.spread(k, at)
            p.give(at)
    hook()

    def arrive(p, k):
        for name, step in (("v+", -1), ("v-", 1)):
            p.wait((name, k))
            at = (offset[k], step)
            if (name == "v+") == (k in (0, 3)):
                p.push(("relay", k), at, (0, -step))
            p.give(at)

    for p in parts:
        arrive(p, 0)
    for p in parts:
        p.wait(("far", 1))
        p.wait(("far", 2))
        p.spread(3, (2, 0))
        p.give((2, 0))
    for k in range(1, len(offset)):
        for p in parts:
            arrive(p, k)
    for k in range(len(offset)):
        for p in parts:
            p.wait(("relay", k))
            p.give((offset[k], 2))


def norm_gather(links, own_slot, gain_buf, which, xbuf, stat, out, base, hook, skip=0):
    own_slot()
    rows, chunk = xbuf.shape[1:]
    tags = itertools.count(base)
    line = [links.send(xbuf.at[0], xbuf.at[NX - dx], links.at_line(dx, 0), next(tags)) for dx in FAR_FIRST]
    yield
    phase = Phases()
    for n, c in enumerate(line):
        phase(f"ng_line{which}_{n}")
        c.wait_recv()
    phase("ng_stats")
    held = xbuf[...].astype(jnp.float32)
    count = NX * chunk
    mean = lane_sum(jnp.sum(held, axis=0)) / count
    dev = held - mean[None]
    square = lane_sum(jnp.sum(dev * dev, axis=0))
    lane = lax.broadcasted_iota(jnp.int32, (rows, 128), 1)
    stat[0] = jnp.where(lane == 0, mean, square)
    links.send(stat.at[0], stat.at[1], links.at_line(0, 1), next(tags)).wait_recv()
    other_mean, other_square = stat[1, :, 0:1], stat[1, :, 1:2]
    both = (mean + other_mean) * 0.5
    gap = mean - other_mean
    var = (square + other_square + gap * gap * (count * 0.5)) / (2 * count)
    scale = lax.rsqrt(var + EPS)
    for e in range(skip, NX):
        out[0, links.slot_rows(0, 0, rows), e * chunk:(e + 1) * chunk] = (
            (xbuf[e].astype(jnp.float32) - both) * scale * gain_buf[e, which:which + 1, :]).astype(jnp.bfloat16)
    phase("ng_plane")
    crossing = Group(links, out.at[1])
    plane_gather(links, out, tags, lambda: hook(crossing), crossing, skip * chunk)
    phase.close()
    yield crossing


def step_kernel(vocab_own, own_rows, hid_ref, gain_a, gain_f, freq_ref, len_ref, k_hbm, v_hbm,
                wq_hbm, wk_hbm, wv_hbm, wo_ref, wg_ref, wu_ref, wd_hbm, emb_ref,
                knew_ref, vnew_ref, z_ref, norm_ref,
                wq_ref, wk_ref, wv_ref, k_buf, v_buf, wd_buf, wo_all, att, rc, gu_acc, n_buf, w_buf, wq_t, wq_buf, sel, sel_t, qx, qr, qy, qf,
                kvp, kvr, o_buf, o_got, o_all, act,
                part, ra1, rb1, ra2, rb2, acc_a, acc_b, xbuf, stat, xbuf2, stat2, gains, f_buf, emb_buf,
                w_relay, emb_relay, row_stats, lse_x, lse_y, send_sem, recv_sem, local_sem):
    links = Links(send_sem, recv_sem)
    phase = Phases()
    f32, bf16 = jnp.float32, jnp.bfloat16
    z, y, xid, yid = links.z, links.y, links.x_idx, links.y_idx
    total_rows, chunk = hid_ref.shape
    rows = total_rows // (NY * NZ)
    here_rows = links.slot_rows(0, 0, rows)
    half = chunk // 2
    nx2, nyz = 2 * NX, NY * NZ
    group = NY * rows
    head = 128
    pad = 8
    partner = links.at_line(0, 1)
    line_id = links.line_id
    gather_tags = len(HOPS) + 1 + len(PLANE) * CORES + CORES
    gather_base = [next(links.tags) for _ in range(gather_tags)][0]

    def dot(a, b):
        return jnp.dot(a, b, preferred_element_type=f32)

    def dot_t(a, b):
        return lax.dot_general(a, b, NT, preferred_element_type=f32)

    def rest(ref, n):
        return Group(links, ref.at[0:n - 1])

    local = []

    def fetch(src, dst):
        copy = pltpu.make_async_copy(src, dst, local_sem.at[len(local)])
        copy.start()
        local.append(copy)
        return copy

    ff = wg_ref.shape[1] // nx2

    def w_piece(ref, dx, oc):
        return ref.at[:, pl.ds(pl.multiple_of(line_id(dx, oc) * ff, ff), ff)]

    def w_slot(which, dx, oc):
        back = (NX - dx) % NX
        return w_buf.at[int(oc), pl.ds(back * chunk, chunk), pl.ds(which * ff, ff)]

    take = emb_buf.shape[1]

    def emb_start(xi):
        return pl.multiple_of(vocab_own * xi // pad * pad, pad)

    def emb_piece(dx, oc):
        return emb_ref.at[pl.ds(emb_start(line_id(dx, oc)), take), :]

    def emb_slot(dx, oc):
        return emb_buf.at[int(oc), :, pl.ds((NX - dx) % NX * chunk, chunk)]

    near_part = (take // 2 + 15) // 16 * 16
    far_parts = ((0, near_part), (near_part, take - near_part))

    def emb_half(oc, way):
        first, size = far_parts[way]
        return emb_ref.at[pl.ds(pl.multiple_of(emb_start(line_id(2, oc)) + first, pad), size), :]

    def emb_mid(oc, way):
        return emb_relay.at[way, oc, pl.ds(0, far_parts[way][1])]

    def emb_far_slot(oc, way):
        return emb_buf.at[int(oc), pl.ds(*far_parts[way]), pl.ds(2 * chunk, chunk)]

    got_wq = fetch(wq_hbm, wq_ref)
    own_w = [fetch(w_piece(wg_ref, 0, 0), w_slot(0, 0, 0)), fetch(w_piece(wu_ref, 0, 0), w_slot(1, 0, 0))]
    got_kv = [fetch(k_hbm, k_buf), fetch(v_hbm, v_buf)]
    got_wkv = [fetch(wk_hbm, wk_ref), fetch(wv_hbm, wv_ref)]
    got_wd = fetch(wd_hbm, wd_buf)
    own_emb = fetch(emb_piece(0, 0), emb_slot(0, 0))

    qc = wq_ref.shape[1]
    qs = qc // nx2
    per = head // qs
    wq_buf[...] = jnp.zeros(wq_buf.shape, bf16)

    phase("row_stats")
    eye = lax.broadcasted_iota(jnp.int32, (head, head), 0) == lax.broadcasted_iota(jnp.int32, (head, head), 1)
    blocks = total_rows // head

    def block_rows(b):
        return slice(b * head, (b + 1) * head)

    def to_row(v):
        return jnp.sum(jnp.where(eye, v, 0.0), axis=0, keepdims=True)

    def to_col(v):
        return lane_sum(jnp.where(eye, v, 0.0))

    row_stats[xid] = jnp.zeros((2 * pad, head), f32)
    for b in range(blocks):
        held = hid_ref[block_rows(b), :].astype(f32)
        mean = lane_sum(held) / chunk
        dev = held - mean
        row_stats[xid, b:b + 1, :] = to_row(mean)
        row_stats[xid, pad + b:pad + b + 1, :] = to_row(lane_sum(dev * dev))

    phase("barrier")
    links.barrier()

    phase("front_send")
    gains[0, 0:1, :] = gain_a[...]
    gains[0, 1:2, :] = gain_f[...]
    gains[0, 2:, :] = jnp.zeros((6, chunk), f32)

    def own_input():
        xbuf[0] = hid_ref[here_rows, :]

    w_far, emb_far = [], []
    w_got = [Group(links, w_buf.at[0, 0:2 * chunk]), Group(links, w_buf.at[1, 0:(NX - 1) * chunk])]
    w_last = Group(links, w_buf.at[0, 0:2 * chunk])
    emb_got = [Group(links, emb_buf.at[0, :, 0:(NX - 1) * chunk]), Group(links, emb_buf.at[1])]
    ways = [(way, hop, oc) for oc in (0, 1) for way, hop in enumerate(HOPS[:2])]

    def forward_weights():
        for (way, hop, oc), c in zip(ways, w_far):
            c.wait_recv()
            w_last.send(w_relay.at[way, oc], w_buf.at[oc, pl.ds(2 * chunk, chunk), pl.ds(way * ff, ff)],
                        links.at_line(hop, oc))

    def emb_out(some):
        for way, hop, oc in some:
            emb_far.append(links.send(emb_half(oc, way), emb_mid(oc, way), links.at_line(hop, 0), long=True))

    def emb_on(some, arrived):
        for (way, hop, oc), c in zip(some, arrived):
            c.wait_recv()
            emb_got[oc].send(emb_mid(oc, way), emb_far_slot(oc, way), links.at_line(hop, oc))

    def amid(crossing):
        forward_weights()
        stats_got.wait()
        means = row_stats[:, :pad, :]
        mean = jnp.sum(means, axis=0) / nx2
        gap = means - mean[None]
        square = jnp.sum(row_stats[:, pad:, :], axis=0) + jnp.sum(gap * gap, axis=0) * chunk
        scale = lax.rsqrt(square / (nx2 * chunk) + EPS)
        for b in range(blocks):
            n_buf[0, block_rows(b), 0:chunk] = (
                (hid_ref[block_rows(b), :].astype(f32) - to_col(mean[b:b + 1, :])) * to_col(scale[b:b + 1, :])
                * gains[0, 0:1, :]).astype(bf16)
        own = n_buf.at[0, :, 0:chunk]
        crossing.send(own, n_buf.at[1, :, 0:chunk], partner)

    front = norm_gather(links, own_input, gains, 0, xbuf, stat, n_buf, gather_base, amid, skip=1)
    next(front)
    gain_got = rest(gains, NX)
    for dx in HOPS:
        gain_got.send(gains.at[0], gains.at[NX - dx], links.at_line(dx, 0))
    stats_got = rest(row_stats, nx2)
    for p in LINE:
        stats_got.send(row_stats.at[xid], row_stats.at[xid], links.at_line(*p))
    for way, hop, oc in ways:
        w_far.append(links.send(w_piece((wg_ref, wu_ref)[way], 2, oc), w_relay.at[way, oc], links.at_line(hop, 0),
                                long=True))

    got_wq.wait()
    eye_q = (lax.broadcasted_iota(jnp.int32, (qc, qc), 0) == lax.broadcasted_iota(jnp.int32, (qc, qc), 1))
    wq_t[...] = dot_t(eye_q.astype(bf16), wq_ref[...]).astype(bf16)
    wq_buf[0, 0:qs, 0:chunk] = wq_t[pl.ds(pl.multiple_of(xid * qs, qs), qs), :]

    def wq_rows(dx, oc):
        return wq_t.at[pl.ds(pl.multiple_of(line_id(dx, oc) * qs, qs), qs), :]

    def wq_slot(dx, oc):
        return wq_buf.at[oc, pl.ds(0, qs), pl.ds((NX - dx) % NX * chunk, chunk)]

    wq_got = Group(links, wq_t.at[0:qc - qs])
    for dx, oc in LINE:
        wq_got.send(wq_rows(dx, oc), wq_slot(dx, oc), links.at_line(dx, oc))
    for which, ref in enumerate((wg_ref, wu_ref)):
        for dx, oc in LINE[:1] + NEAR:
            w_got[oc].send(w_piece(ref, dx, oc), w_slot(which, dx, oc), links.at_line(dx, oc))

    phase("selections")
    r_id = lax.broadcasted_iota(jnp.int32, (nx2 * nyz * pad, 1), 0)
    r_j = r_id % pad
    r_src = jnp.where(r_j < own_rows, r_id // pad % nyz * rows + r_id // (pad * nyz) * own_rows + r_j, -1)
    s_id = lax.broadcasted_iota(jnp.int32, (1, total_rows), 1)
    sel[...] = jnp.where(r_src == s_id, 1.0, 0.0).astype(bf16)
    t_id = lax.broadcasted_iota(jnp.int32, (group, 1), 0)
    t_in = t_id % rows
    t_src = t_in // own_rows * (NY * pad) + t_id // rows * pad + t_in % own_rows
    u_id = lax.broadcasted_iota(jnp.int32, (1, nx2 * NY * pad), 1)
    sel_t[...] = jnp.where(t_src == u_id, 1.0, 0.0).astype(bf16)
    k_id = lax.broadcasted_iota(jnp.int32, (nx2 * pad, rows), 0)
    k_src = jnp.where(k_id % pad < own_rows, k_id // pad * own_rows + k_id % pad, -1)
    sel_kv = jnp.where(k_src == lax.broadcasted_iota(jnp.int32, (nx2 * pad, rows), 1), 1.0, 0.0).astype(bf16)

    phase.close()
    gain_got.wait()
    lane = lax.broadcasted_iota(jnp.int32, (1, head), 1)
    lengths = []
    for b in range(own_rows):
        index = (yid * nx2 + xid) * own_rows + b
        row = len_ref[pl.ds(index // head, 1), :].astype(f32)
        lengths.append(lane_sum(jnp.where(lane == index % head, row, 0.0)))
    lengths = jnp.concatenate(lengths + lengths[:pad - own_rows], axis=0)
    angles = lengths * freq_ref[...]
    cos_all = jnp.cos(angles)
    sin_all = jnp.sin(angles) * jnp.where(lane < head // 2, -1.0, 1.0)

    crossing = next(front)
    phase("ng_cross")
    crossing.wait()
    phase("kv_part")

    for c in got_wkv:
        c.wait()
    n_own = dot(sel_kv, n_buf[0, links.slot_rows(0, 0, rows), 0:chunk]).astype(bf16)
    kvp[:, :, :head] = dot(n_own, wk_ref[...]).reshape(nx2, pad, head)
    kvp[:, :, head:] = dot(n_own, wv_ref[...]).reshape(nx2, pad, head)
    kv_got = rest(kvr, nx2)
    for p in LINE:
        kv_got.send(kvp.at[line_id(*p)], kvr.at[xid], links.at_line(*p))
    kvr[xid] = kvp[xid]

    phase("wait_wq")
    wq_got.wait()
    phase("q_mm")
    q_all = jnp.concatenate([
        (dot_t(n_buf[0, i * group:(i + 1) * group, :], wq_buf[0])
         + dot_t(n_buf[1, i * group:(i + 1) * group, :], wq_buf[1])).astype(bf16) for i in range(NZ)], axis=0)
    span = nyz * pad
    for i in range(nx2):
        chosen = dot(sel[i * span:(i + 1) * span, :], q_all)
        quarter = span // per
        packed = chosen[:quarter, :]
        for g in range(1, per):
            packed = packed + pltpu.roll(chosen[g * quarter:(g + 1) * quarter, :], g * qs, 1)
        qx[i] = packed.astype(bf16)
    q_got = rest(qr, nx2)
    for p in LINE:
        q_got.send(qx.at[line_id(*p)], qr.at[xid], links.at_line(*p))
    qr[xid] = qx[xid]

    phase("wait_w")
    for c in own_w:
        c.wait()
    for c in w_got:
        c.wait()
    phase("gate_up")

    def act_at(k, dx):
        return act.at[(z + k) % NZ, :, pl.ds(pl.multiple_of(line_id(dx, 0) * ff, ff), ff)]

    def act_out(k, dx, to_dx):
        return links.send(act_at(k, dx), act_at(k, dx), links.at_line(to_dx, 0))

    def act_give(k, dx):
        cross[k].send(act_at(k, dx), act_at(k, dx), partner)

    turns = (2, 1, 3, 0)
    early, late = turns[:2], turns[2:]
    near_act, far_act = {}, {}
    cross = {k: Group(links, act.at[0, :, 0:NX * ff]) for k in turns}
    def group_rows(k):
        return pl.ds(pl.multiple_of((z + k) % NZ * group, group), group)

    far = slice(2 * chunk, (NX - 1) * chunk)

    def over(k, part_cols):
        return dot(n_buf[0, group_rows(k), part_cols], w_buf[0, part_cols, :]) + dot(
            n_buf[1, group_rows(k), part_cols], w_buf[1, part_cols, :])

    for k in turns:
        gu_acc[k] = over(k, slice(0, far.start)) + over(k, slice(far.stop, NX * chunk))
    phase("wait_w_far")
    w_last.wait()
    phase("gate_up_far")
    for k in turns:
        both = (gu_acc[k] + over(k, far)).astype(bf16).astype(f32)
        gate, up = both[:, :ff], both[:, ff:]
        act_at(k, 0)[...] = (gate * jax.nn.sigmoid(gate) * up).astype(bf16)
        near_act[k] = [(dx, act_out(k, 0, dx)) for dx in HOPS[:2]]
        act_give(k, 0)

    def act_pass(k):
        for dx, c in near_act[k]:
            c.wait_recv()
            if (k in early) == (dx == 1):
                far_act[k] = act_out(k, NX - dx, dx)
            act_give(k, NX - dx)

    low, high = pl.ds(0, half), pl.ds(half, half)
    first_a, first_b = Group(links, ra1), Group(links, rb1)

    def act_use(k):
        cross[k].wait()
        g = (z + k) % NZ
        part[g] = dot(act[g], wd_buf[...]).reshape(NY, rows, chunk)
        if k:
            first_b.send(part.at[g, :, :, high], rb1.at[k - 1], links.at_plane(k, 0))

    def along_y(k):
        g = (z + k) % NZ
        for d in early + late[:1]:
            first_a.send(part.at[g, (y + d) % NY, :, low], ra1.at[d - 1, g], links.at_plane(0, d))

    def act_far(ks):
        for k in ks:
            far_act[k].wait_recv()
            act_give(k, 2)

    phase("wait_q")
    q_got.wait()
    phase("q_sum")
    lane_group = lax.broadcasted_iota(jnp.int32, (1, head), 1) // qs
    for j in range(qc // head):
        came = [qr[j * per + i].astype(f32) for i in range(per)]
        for g in range(per):
            piece = jnp.zeros((span // per, head), f32)
            for i in range(per):
                piece = piece + jnp.where(lane_group == i, pltpu.roll(came[i], (i - g) % per * qs, 1), 0.0)
            qy[g * per:(g + 1) * per, :, j * head:(j + 1) * head] = piece.reshape(per, pad, head)

    def plane_id(dz, dy):
        return (z + dz) % NZ * NY + (y + dy) % NY

    y_got = rest(qf, nyz)
    for p in PLANE:
        y_got.send(qy.at[plane_id(*p)], qf.at[yid], links.at_plane(*p))
    qf[yid] = qy[yid]

    def wo_rows(dz):
        return wo_all.at[pl.ds(pl.multiple_of((z + dz) % NZ * qc, qc), qc), :]

    wo_got = Group(links, wo_all.at[0:(NZ - 1) * qc])
    for d in HOPS:
        wo_got.send(wo_ref, wo_rows(0), links.at_plane(d, 0))
    own_wo = fetch(wo_ref, wo_rows(0))

    phase("act_pass")
    for k in early:
        act_pass(k)
    phase("wait_kv")
    kv_got.wait()
    kv_sum = kvr[0]
    for i in range(1, nx2):
        kv_sum = kv_sum + kvr[i]
    kv_new = kv_sum.astype(bf16).astype(f32)

    def turn(v, b=None):
        cos, sin = (cos_all, sin_all) if b is None else (cos_all[b:b + 1, :], sin_all[b:b + 1, :])
        return (v * cos + pltpu.roll(v, head // 2, 1) * sin).astype(bf16)

    k_new = turn(kv_new[:, :head])
    knew_ref[...] = k_new
    vnew_ref[...] = kv_new[:, head:].astype(bf16)
    k_row, v_row = k_new.astype(f32), kv_new[:, head:]
    phase("act_pass2")
    for k in late:
        act_pass(k)
    emb_out(ways[:2])
    phase("wait_qy")
    for c in got_kv:
        c.wait()
    y_got.wait()
    phase("attention")
    seq = k_buf.shape[1]
    score_scale = head ** -0.5
    position = lax.broadcasted_iota(jnp.int32, (1, seq), 1).astype(f32)
    o_buf[...] = jnp.zeros(o_buf.shape, f32)
    for b in range(own_rows):
        q_b = jnp.concatenate([turn(qf[:, b, j * head:(j + 1) * head], b) for j in range(qc // head)], axis=0)
        scores = dot_t(q_b, k_buf[b]) * score_scale
        score_new = lane_sum(q_b.astype(f32) * k_row[b:b + 1, :]) * score_scale
        valid = position < lengths[b:b + 1, :]
        top = jnp.maximum(jnp.max(jnp.where(valid, scores, -jnp.inf), axis=-1, keepdims=True), score_new)
        weights = jnp.where(valid, jnp.exp(scores - top), 0.0)
        weight_new = jnp.exp(score_new - top)
        denom = lane_sum(weights) + weight_new
        o_b = dot((weights / denom).astype(bf16), v_buf[b])
        o_b = o_b + (weight_new / denom).astype(bf16).astype(f32) * v_row[b:b + 1, :]
        o_b = o_b.astype(bf16).astype(f32)
        for j in range(qc // head):
            o_buf[:, :, b, j * head:(j + 1) * head] = o_b[j * nyz:(j + 1) * nyz, :].reshape(NZ, NY, head)
    o_back = rest(o_got, NY)
    for d in HOPS:
        o_back.send(o_buf.at[:, (y + d) % NY], o_got.at[y], links.at_plane(0, d))
    phase("act_early")
    act_far(turns)
    got_wd.wait()
    for k in turns:
        act_use(k)
        along_y(k)
    o_got[y] = o_buf[:, y]

    phase("wait_oy")
    o_back.wait()
    for i in range(NZ):
        o_all[xid, :, i * qc:(i + 1) * qc] = o_got[:, i].reshape(NY * pad, qc).astype(bf16)
    o_here = o_all.at[xid]
    o_line = [links.send(o_here, o_here, links.at_line(dx, 0)) for dx in HOPS]
    o_cross = rest(o_all, NX + 1)
    o_cross.send(o_here, o_here, partner)
    emb_out(ways[2:])
    emb_got[1].send(emb_piece(0, 1), emb_slot(0, 1), partner)
    emb_on(ways[:2], emb_far[:2])
    phase("wait_o")
    for dx, c in zip(HOPS, o_line):
        c.wait_recv()
        came = o_all.at[line_id(NX - dx, 0)]
        o_cross.send(came, came, partner)
    wo_got.wait()
    own_wo.wait()
    o_cross.wait()
    phase("out_mm")
    o_nat = dot(sel_t[...], o_all[...].reshape(nx2 * NY * pad, NZ * qc)).astype(bf16)
    att[...] = dot(o_nat, wo_all[...]).reshape(NY, rows, chunk)
    att_got = Group(links, rc)
    for d in HOPS:
        att_got.send(att.at[(y + d) % NY], rc.at[d - 1], links.at_plane(0, d))

    phase("wait_rs1")
    first_b.wait()
    acc_b[...] = (part[z, :, :, half:] + rb1[0]) + (rb1[1] + rb1[2])
    second = [Group(links, rb2), Group(links, ra2)]
    for d in HOPS:
        second[0].send(acc_b.at[(y + d) % NY], rb2.at[d - 1], links.at_plane(0, d))
    phase("wait_rs1a")
    first_a.wait()
    acc_a[...] = (part[:, y, :, :half] + ra1[0]) + (ra1[1] + ra1[2])
    for d in HOPS:
        second[1].send(acc_a.at[(z + d) % NZ], ra2.at[d - 1], links.at_plane(d, 0))
    phase("wait_att")
    att_got.wait()
    phase("wait_rs2")
    for c in second:
        c.wait()
    phase("rs_sum2")
    def own_residual():
        res = hid_ref[here_rows, :].astype(f32) + ((att[y] + rc[0]) + (rc[1] + rc[2]))
        xbuf2[0, :, :half] = res[:, :half] + ((acc_a[z] + ra2[0]) + (ra2[1] + ra2[2]))
        xbuf2[0, :, half:] = res[:, half:] + ((acc_b[y] + rb2[0]) + (rb2[1] + rb2[2]))

    back = norm_gather(links, own_residual, gains, 1, xbuf2, stat2, f_buf, gather_base, lambda crossing: None)
    next(back)
    emb_on(ways[2:], emb_far[2:])
    for dx, oc in NEAR:
        emb_got[oc].send(emb_piece(dx, oc), emb_slot(dx, oc), links.at_line(dx, oc))
    phase.close()
    crossing = next(back)
    phase("wait_emb")
    own_emb.wait()
    for c in emb_got:
        c.wait()

    phase("logits")
    wide_n = 256
    for h in range(CORES):
        if h:
            crossing.wait()
        for i in range(total_rows // wide_n):
            cols = slice(i * wide_n, (i + 1) * wide_n)
            term = dot_t(emb_buf[h], f_buf[h, cols, :])
            z_ref[:, cols] = z_ref[:, cols] + term if h else term

    phase("lse_own")
    shift = vocab_own * xid - emb_start(xid)
    vid = lax.broadcasted_iota(jnp.int32, (take, 1), 0)
    own = (vid >= shift) & (vid < shift + vocab_own)
    for b in range(blocks):
        zb = jnp.where(own, z_ref[:, b * 128:(b + 1) * 128], -jnp.inf)
        top = jnp.max(zb, axis=0, keepdims=True)
        lse_x[xid, b:b + 1, :] = top
        lse_x[xid, 8 + b:9 + b, :] = jnp.sum(jnp.exp(zb - top), axis=0, keepdims=True)
    for b in range(blocks, 8):
        lse_x[xid, b:b + 1, :] = jnp.zeros((1, 128), f32)
        lse_x[xid, 8 + b:9 + b, :] = jnp.ones((1, 128), f32)

    def merge(ref):
        tops = ref[:, :8, :]
        top = jnp.max(tops, axis=0)
        return top, jnp.sum(ref[:, 8:, :] * jnp.exp(tops - top[None]), axis=0)

    phase("lse_line")
    got = rest(lse_x, nx2)
    for p in LINE:
        got.send(lse_x.at[xid], lse_x.at[xid], links.at_line(*p))
    got.wait()
    top, mass = merge(lse_x)
    lse_y[yid, :8, :] = top
    lse_y[yid, 8:, :] = mass
    phase("lse_plane")
    got = rest(lse_y, nyz)
    for p in PLANE:
        got.send(lse_y.at[yid], lse_y.at[yid], links.at_plane(*p))
    got.wait()
    top, mass = merge(lse_y)
    norm_ref[...] = top + jnp.log(mass)
    phase("finish")
    links.finish()
    phase.close()


def whole_step(hidden, freq, lens, k_cache, v_cache, g_attn, w_query, w_key, w_value,
               w_gate, w_up, w_out, w_down, g_final, embedding):
    total_rows, chunk = hidden.shape
    own_rows, seq, head = k_cache.shape
    rows = total_rows // (NY * NZ)
    vocab_own = embedding.shape[0] // (2 * NX)
    take = (vocab_own + 6 + 15) // 16 * 16
    half = chunk // 2
    qc = w_query.shape[1]
    ff = w_gate.shape[1] // (2 * NX)
    f32, bf16 = jnp.float32, jnp.bfloat16
    nyz, nx2, pad = NY * NZ, 2 * NX, 8
    vmem = pl.BlockSpec(memory_space=pltpu.VMEM)
    hbm = pl.BlockSpec(memory_space=pl.ANY)
    V = pltpu.VMEM
    return pl.pallas_call(
        lambda *refs: step_kernel(vocab_own, own_rows, *refs),
        out_shape=(jax.ShapeDtypeStruct((pad, head), bf16), jax.ShapeDtypeStruct((pad, head), bf16),
                   jax.ShapeDtypeStruct((take, total_rows), f32), jax.ShapeDtypeStruct((pad, head), f32)),
        in_specs=[vmem] * 5 + [hbm] * 10,
        out_specs=(vmem,) * 4,
        scratch_shapes=[
            V((chunk, qc), bf16), V((chunk, head), bf16), V((chunk, head), bf16),
            V((own_rows, seq, head), bf16), V((own_rows, seq, head), bf16),
            V((nx2 * ff, chunk), bf16), V((NZ * qc, chunk), bf16), V((NY, rows, chunk), f32), V((3, rows, chunk), f32),
            V((NZ, NY * rows, 2 * ff), f32), V((2, total_rows, NX * chunk), bf16), V((2, NX * chunk, 2 * ff), bf16),
            V((qc, chunk), bf16), V((2, head, NX * chunk), bf16),
            V((nx2 * nyz * pad, total_rows), bf16), V((NY * rows, nx2 * NY * pad), bf16),
            V((nx2, nyz * pad // 4, head), bf16), V((nx2, nyz * pad // 4, head), bf16),
            V((nyz, pad, qc), f32), V((nyz, pad, qc), f32),
            V((nx2, pad, 2 * head), f32), V((nx2, pad, 2 * head), f32),
            V((NZ, NY, pad, qc), f32), V((NY, NZ, pad, qc), f32), V((nx2, NY * pad, NZ * qc), bf16),
            V((NZ, NY * rows, nx2 * ff), bf16),
            V((NZ, NY, rows, chunk), f32),
            V((3, NZ, rows, half), f32), V((3, NY, rows, half), f32), V((3, rows, half), f32), V((3, rows, half), f32),
            V((NZ, rows, half), f32), V((NY, rows, half), f32),
            V((NX, rows, chunk), bf16), V((2, rows, 128), f32), V((NX, rows, chunk), f32), V((2, rows, 128), f32),
            V((NX, 8, chunk), f32),
            V((2, total_rows, NX * chunk), bf16), V((2, take, NX * chunk), bf16),
            V((2, 2, chunk, ff), bf16), V((2, 2, (take // 2 + 15) // 16 * 16, chunk), bf16),
            V((nx2, 16, 128), f32), V((nx2, 16, 128), f32), V((nyz, 16, 128), f32),
            pltpu.SemaphoreType.DMA((SENDS,)), pltpu.SemaphoreType.DMA((TAGS,)), pltpu.SemaphoreType.DMA((10,)),
        ],
        compiler_params=pltpu.CompilerParams(
            collective_id=1, has_side_effects=True, vmem_limit_bytes=60 << 20),
        name="decode_step",
    )(hidden, g_attn[None, :], g_final[None, :], freq, lens, k_cache, v_cache,
      w_query, w_key, w_value, w_out, w_gate, w_up, w_down, embedding)


def solution(mesh):
    row_spec = P(("dp", "yax", "xax"))

    def local_step(hidden, cache_len, k_cache, v_cache, g_attn, w_query, w_key, w_value,
                   w_gate, w_up, w_out, w_down, g_final, embedding):
        rows = hidden.shape[0]
        half_dim = k_cache.shape[2] // 2
        inv_freq = ROPE_BASE ** (-(np.arange(half_dim, dtype=np.float64) * 2.0) / (2 * half_dim))
        freq = np.concatenate([inv_freq, inv_freq])[None, :].astype(np.float32)
        key_own, value_own, logits_wide, norm_tile = whole_step(
            hidden, freq, cache_len.reshape(rows // 128, 128), k_cache, v_cache, g_attn, w_query, w_key, w_value,
            w_gate, w_up, w_out, w_down, g_final, embedding)
        own_rows = k_cache.shape[0]
        vocab_own = embedding.shape[0] // (CORES * NX)
        first = vocab_own * lax.axis_index("xax")
        logits = lax.dynamic_slice_in_dim(logits_wide, first - first // 8 * 8, vocab_own, axis=0)
        log_norm = norm_tile[:rows // 128].reshape(rows)
        return key_own[:own_rows], value_own[:own_rows], (logits - log_norm).T, log_norm

    in_specs = (P("dp", "xax"), P("dp"), row_spec, row_spec, P("xax"), P("xax", "yax"),
                P("xax"), P("xax"), P("xax", "yax"), P("xax", "yax"),
                P("yax", "xax"), P("yax", "xax"), P("xax"), P("yax", "xax"))
    out_specs = (row_spec, row_spec, P("dp", ("yax", "xax")), P("dp"))
    return jax.shard_map(local_step, mesh=mesh, in_specs=in_specs, out_specs=out_specs, check_vma=False)
```

profile of v0, /device:TPU:1, one launch (start us, length us, event | category | flops | bytes accessed | tf_op | source)
XLA Modules:
  0.0 120.4 jit_solution(15337915070179882592)
XLA Ops:
  0.7 115.5 %decode_step.1 = (bf16[8,128]{1,0:T(8,128)(2,1)}, bf16[8,128]{1,0:T(8,128)(2,1)}, f32[400,768]{1,0:T(8,128)}, f32[8,128]{1,0:T(8,128)}) custom-call(bf16[768,512]{1,0:T(8,128)(2,1)} %refs_0_.1, f32[1,512]{1,0:T(1,128)} %bitcast.10, f32[1,512]{1,0:T(1,128)} %bitcast.11, f32[1,128]{1,0:T(1,128)} %constant.28.clone.refs_3_, s32[6,128]{1,0:T(8,128)} %bitcast.9, ...), custom_call_target="tpu_custom_call" | custom-call | tf_op jit(solution)/shard_map/decode_step/pallas_call | solution.py:741
  116.1 0.7 slice_bitcast_fusion
  116.8 0.0 copy-start
  116.8 0.0 copy-start.2
  116.8 0.0 copy-start.1
  116.8 2.5 %subtract_bitcast_fusion = f32[768,394]{0,1:T(8,128)} fusion(f32[400,768]{1,0:T(8,128)} %get-tuple-element.10, s32[]{:T(128)S(6)} %select_n.9, f32[768]{0:T(1024)S(1)} %slice_bitcast_fusion), kind=kLoop, calls=%fused_computation | loop fusion | flops 302592 | bytes 2423812 | tf_op jit(solution)/shard_map/transpose | solution.py:793
  119.3 0.0 copy-done
  119.3 0.0 copy-done.2
  119.3 0.6 copy.21
  119.9 0.0 copy-done.1
  119.9 0.6 copy.22
Async XLA Ops:
  116.8 2.5 %copy-start = (f32[768]{0:T(1024)}, f32[768]{0:T(1024)S(1)}, u32[]{:S(2)}) copy-start(f32[768]{0:T(1024)S(1)} %slice_bitcast_fusion) | copy-start | bytes 9220
  116.8 2.5 %copy-start.2 = (bf16[8,128]{1,0:T(8,128)(2,1)S(1)}, bf16[8,128]{1,0:T(8,128)(2,1)}, u32[]{:S(2)}) copy-start(bf16[8,128]{1,0:T(8,128)(2,1)} %get-tuple-element.8) | copy-start | bytes 6148
  116.8 3.0 %copy-start.1 = (bf16[8,128]{1,0:T(8,128)(2,1)S(1)}, bf16[8,128]{1,0:T(8,128)(2,1)}, u32[]{:S(2)}) copy-start(bf16[8,128]{1,0:T(8,128)(2,1)} %get-tuple-element.9) | copy-start | bytes 6148
where the time goes:
time: 121 us; the launch traced here: 120 us
  Pallas kernels  115 us (95%)
  other arithmetic  2.45 us (2%)
  local copies, waits for them, and re-layouts  1.85 us (2%)
    pallas_call x1, Pallas kernels, whole_step(): pl.pallas_call(lambda *refs: step_kernel(vocab_own, own_rows, *refs), out...  115 us
    transpose x1, other arithmetic, local_step(): return (key_own[:own_rows], value_own[:own_rows], (logits - log_norm).T,...  2.45 us

commit v1 on v0

--- a/solution.py
+++ b/solution.py
@@ -14,7 +14,7 @@
 MESH_ID = pl.DeviceIdType.MESH
 NY = NZ = NX = 4
 CORES = 2
-POOL, SENDS, TAGS = 24, 59, 86
+POOL, SENDS, TAGS = 24, 59, 89
 HOPS = (1, 3, 2)
 FAR_FIRST = (2, 1, 3)
 LINE = [(0, 1), (1, 0), (3, 0), (1, 1), (3, 1), (2, 0), (2, 1)]
@@ -110,7 +110,7 @@
     return jnp.sum(v, axis=-1, keepdims=True)
 
 
-def plane_gather(links, buf, tags, hook, crossing, start):
+def plane_gather(links, buf, tags, hooks, crossing, start):
     cols = buf.shape[-1]
     rows = buf.shape[1] // (NY * NZ)
     span = (cols - start) // 2
@@ -150,6 +150,7 @@
         p.spread(0, (0, 0))
     for p in parts:
         p.give((0, 0))
+    hooks[0](crossing)
     for k, name in enumerate(("u+", "u-"), 1):
         for p in parts:
             p.wait(name)
@@ -157,7 +158,7 @@
             p.push(("far", k), at, (-offset[k], 0), piece=k - 1)
             p.spread(k, at)
             p.give(at)
-    hook()
+    hooks[1]()
 
     def arrive(p, k):
         for name, step in (("v+", -1), ("v-", 1)):
@@ -183,11 +184,13 @@
             p.give((offset[k], 2))
 
 
-def norm_gather(links, own_slot, gain_buf, which, xbuf, stat, out, base, hook, skip=0):
-    own_slot()
+def norm_gather(links, own_slot, gain_buf, which, xbuf, stat, out, base, hooks, skip=0):
     rows, chunk = xbuf.shape[1:]
     tags = itertools.count(base)
-    line = [links.send(xbuf.at[0], xbuf.at[NX - dx], links.at_line(dx, 0), next(tags)) for dx in FAR_FIRST]
+    line = []
+    for cols in own_slot():
+        line += [links.send(xbuf.at[0, :, cols], xbuf.at[NX - dx, :, cols], links.at_line(dx, 0), next(tags))
+                 for dx in FAR_FIRST]
     yield
     phase = Phases()
     for n, c in enumerate(line):
@@ -212,15 +215,15 @@
             (xbuf[e].astype(jnp.float32) - both) * scale * gain_buf[e, which:which + 1, :]).astype(jnp.bfloat16)
     phase("ng_plane")
     crossing = Group(links, out.at[1])
-    plane_gather(links, out, tags, lambda: hook(crossing), crossing, skip * chunk)
+    plane_gather(links, out, tags, hooks, crossing, skip * chunk)
     phase.close()
     yield crossing
 
 
 def step_kernel(vocab_own, own_rows, hid_ref, gain_a, gain_f, freq_ref, len_ref, k_hbm, v_hbm,
                 wq_hbm, wk_hbm, wv_hbm, wo_ref, wg_ref, wu_ref, wd_hbm, emb_ref,
-                knew_ref, vnew_ref, z_ref, norm_ref,
-                wq_ref, wk_ref, wv_ref, k_buf, v_buf, wd_buf, wo_all, att, rc, gu_acc, n_buf, w_buf, wq_t, wq_buf, sel, sel_t, qx, qr, qy, qf,
+                knew_ref, vnew_ref, z_hbm, norm_ref,
+                z_ref, wq_ref, wk_ref, wv_ref, k_buf, v_buf, wd_buf, wo_all, att, rc, gu_acc, n_buf, w_buf, wq_t, wq_buf, sel, sel_t, qx, qr, qy, qf,
                 kvp, kvr, o_buf, o_got, o_all, act,
                 part, ra1, rb1, ra2, rb2, acc_a, acc_b, xbuf, stat, xbuf2, stat2, gains, f_buf, emb_buf,
                 w_relay, emb_relay, row_stats, lse_x, lse_y, send_sem, recv_sem, local_sem):
@@ -238,7 +241,7 @@
     pad = 8
     partner = links.at_line(0, 1)
     line_id = links.line_id
-    gather_tags = len(HOPS) + 1 + len(PLANE) * CORES + CORES
+    gather_tags = 2 * len(HOPS) + 1 + len(PLANE) * CORES + CORES
     gather_base = [next(links.tags) for _ in range(gather_tags)][0]
 
     def dot(a, b):
@@ -334,6 +337,7 @@
 
     def own_input():
         xbuf[0] = hid_ref[here_rows, :]
+        yield pl.ds(0, chunk)
 
     w_far, emb_far = [], []
     w_got = [Group(links, w_buf.at[0, 0:2 * chunk]), Group(links, w_buf.at[1, 0:(NX - 1) * chunk])]
@@ -357,7 +361,6 @@
             emb_got[oc].send(emb_mid(oc, way), emb_far_slot(oc, way), links.at_line(hop, oc))
 
     def amid(crossing):
-        forward_weights()
         stats_got.wait()
         means = row_stats[:, :pad, :]
         mean = jnp.sum(means, axis=0) / nx2
@@ -371,7 +374,7 @@
         own = n_buf.at[0, :, 0:chunk]
         crossing.send(own, n_buf.at[1, :, 0:chunk], partner)
 
-    front = norm_gather(links, own_input, gains, 0, xbuf, stat, n_buf, gather_base, amid, skip=1)
+    front = norm_gather(links, own_input, gains, 0, xbuf, stat, n_buf, gather_base, (amid, forward_weights), skip=1)
     next(front)
     gain_got = rest(gains, NX)
     for dx in HOPS:
@@ -655,15 +658,17 @@
     phase("wait_att")
     att_got.wait()
     phase("wait_rs2")
-    for c in second:
-        c.wait()
-    phase("rs_sum2")
+
     def own_residual():
         res = hid_ref[here_rows, :].astype(f32) + ((att[y] + rc[0]) + (rc[1] + rc[2]))
+        second[0].wait()
+        xbuf2[0, :, half:] = res[:, half:] + ((acc_b[y] + rb2[0]) + (rb2[1] + rb2[2]))
+        yield high
+        second[1].wait()
         xbuf2[0, :, :half] = res[:, :half] + ((acc_a[z] + ra2[0]) + (ra2[1] + ra2[2]))
-        xbuf2[0, :, half:] = res[:, half:] + ((acc_b[y] + rb2[0]) + (rb2[1] + rb2[2]))
-
-    back = norm_gather(links, own_residual, gains, 1, xbuf2, stat2, f_buf, gather_base, lambda crossing: None)
+        yield low
+
+    back = norm_gather(links, own_residual, gains, 1, xbuf2, stat2, f_buf, gather_base, (lambda crossing: None, lambda: None))
     next(back)
     emb_on(ways[2:], emb_far[2:])
     for dx, oc in NEAR:
@@ -684,6 +689,8 @@
             cols = slice(i * wide_n, (i + 1) * wide_n)
             term = dot_t(emb_buf[h], f_buf[h, cols, :])
             z_ref[:, cols] = z_ref[:, cols] + term if h else term
+
+    z_out = fetch(z_ref, z_hbm)
 
     phase("lse_own")
     shift = vocab_own * xid - emb_start(xid)
@@ -719,6 +726,7 @@
     top, mass = merge(lse_y)
     norm_ref[...] = top + jnp.log(mass)
     phase("finish")
+    z_out.wait()
     links.finish()
     phase.close()
 
@@ -743,8 +751,9 @@
         out_shape=(jax.ShapeDtypeStruct((pad, head), bf16), jax.ShapeDtypeStruct((pad, head), bf16),
                    jax.ShapeDtypeStruct((take, total_rows), f32), jax.ShapeDtypeStruct((pad, head), f32)),
         in_specs=[vmem] * 5 + [hbm] * 10,
-        out_specs=(vmem,) * 4,
+        out_specs=(vmem, vmem, hbm, vmem),
         scratch_shapes=[
+            V((take, total_rows), f32),
             V((chunk, qc), bf16), V((chunk, head), bf16), V((chunk, head), bf16),
             V((own_rows, seq, head), bf16), V((own_rows, seq, head), bf16),
             V((nx2 * ff, chunk), bf16), V((NZ * qc, chunk), bf16), V((NY, rows, chunk), f32), V((3, rows, chunk), f32),
@@ -764,7 +773,7 @@
             V((2, total_rows, NX * chunk), bf16), V((2, take, NX * chunk), bf16),
             V((2, 2, chunk, ff), bf16), V((2, 2, (take // 2 + 15) // 16 * 16, chunk), bf16),
             V((nx2, 16, 128), f32), V((nx2, 16, 128), f32), V((nyz, 16, 128), f32),
-            pltpu.SemaphoreType.DMA((SENDS,)), pltpu.SemaphoreType.DMA((TAGS,)), pltpu.SemaphoreType.DMA((10,)),
+            pltpu.SemaphoreType.DMA((SENDS,)), pltpu.SemaphoreType.DMA((TAGS,)), pltpu.SemaphoreType.DMA((11,)),
         ],
         compiler_params=pltpu.CompilerParams(
             collective_id=1, has_side_effects=True, vmem_limit_bytes=60 << 20),

time: 121 us -> 120 us (level)
  no operation moved by 1% of the time
where the time goes in v1:
time: 120 us
  Pallas kernels  115 us (96%)
  other arithmetic  2.45 us (2%)
  local copies, waits for them, and re-layouts  1.85 us (2%)
    pallas_call x1, Pallas kernels, whole_step(): pl.pallas_call(lambda *refs: step_kernel(vocab_own, own_rows, *refs), out...  115 us
    transpose x1, other arithmetic, local_step(): return (key_own[:own_rows], value_own[:own_rows], (logits - log_norm).T,...  2.45 us

profile of v1, /device:TPU:1, one launch (start us, length us, event | category | flops | bytes accessed | tf_op | source)
XLA Modules:
  0.0 119.7 jit_solution(3590539072036097745)
XLA Ops:
  0.7 114.7 %decode_step.1 = (bf16[8,128]{1,0:T(8,128)(2,1)}, bf16[8,128]{1,0:T(8,128)(2,1)}, f32[400,768]{1,0:T(8,128)}, f32[8,128]{1,0:T(8,128)}) custom-call(bf16[768,512]{1,0:T(8,128)(2,1)} %refs_0_.1, f32[1,512]{1,0:T(1,128)} %bitcast.10, f32[1,512]{1,0:T(1,128)} %bitcast.11, f32[1,128]{1,0:T(1,128)} %constant.28.clone.refs_3_, s32[6,128]{1,0:T(8,128)} %bitcast.9, ...), custom_call_target="tpu_custom_call" | custom-call | tf_op jit(solution)/shard_map/decode_step/pallas_call | solution.py:749
  115.4 0.7 slice_bitcast_fusion
  116.1 0.0 copy-start
  116.1 0.0 copy-start.2
  116.1 0.0 copy-start.1
  116.1 2.5 %subtract_bitcast_fusion = f32[768,394]{0,1:T(8,128)} fusion(f32[400,768]{1,0:T(8,128)} %get-tuple-element.10, s32[]{:T(128)S(6)} %select_n.9, f32[768]{0:T(1024)S(1)} %slice_bitcast_fusion), kind=kLoop, calls=%fused_computation | loop fusion | flops 302592 | bytes 2423812 | tf_op jit(solution)/shard_map/transpose | solution.py:802
  118.6 0.0 copy-done
  118.6 0.0 copy-done.2
  118.6 0.6 copy.21
  119.1 0.0 copy-done.1
  119.1 0.6 copy.22
Async XLA Ops:
  116.1 2.5 %copy-start = (f32[768]{0:T(1024)}, f32[768]{0:T(1024)S(1)}, u32[]{:S(2)}) copy-start(f32[768]{0:T(1024)S(1)} %slice_bitcast_fusion) | copy-start | bytes 9220
  116.1 2.5 %copy-start.2 = (bf16[8,128]{1,0:T(8,128)(2,1)S(1)}, bf16[8,128]{1,0:T(8,128)(2,1)}, u32[]{:S(2)}) copy-start(bf16[8,128]{1,0:T(8,128)(2,1)} %get-tuple-element.8) | copy-start | bytes 6148
  116.1 3.0 %copy-start.1 = (bf16[8,128]{1,0:T(8,128)(2,1)S(1)}, bf16[8,128]{1,0:T(8,128)(2,1)}, u32[]{:S(2)}) copy-start(bf16[8,128]{1,0:T(8,128)(2,1)} %get-tuple-element.9) | copy-start | bytes 6148
